TPU v7x, 512 devices: a whole 4x8x8 slice. The times are simulated.
512 devices in a mesh: row: 32 (over y_lo, x, core), col: 8 (over z), dp: 2 (over y_hi).
Axes of the slice: x: 4, y: 8 (y_hi: 2, y_lo: 4; y = y_hi * 4 + y_lo), z: 8, core: 2. Of those that a mesh axis runs over, the one named last changes fastest.
Arguments:
- pixels: bfloat16 [2, 3, 1024, 1024], P('dp', None, 'row', 'col'), may hold values from -6 to 6
- cotangent: bfloat16 [2, 256, 256, 1024], P('dp', 'row', 'col'), may hold values from -6 to 6
- embed_weight: bfloat16 [48, 1024], replicated, may hold values from -0.875 to 0.875
- embed_bias: float32 [1024], replicated, may hold values from -4 to 4
- layer_norm_gain: float32 [1024], replicated, may hold values from 0.5 to 1.5
- qkv_weight: bfloat16 [1024, 2304], P('row', ('col', 'dp')), may hold values from -0.1875 to 0.1875
- out_weight: bfloat16 [768, 1024], P('row', ('col', 'dp')), may hold values from -0.21875 to 0.21875
- bias_table: float32 [12, 225], replicated, may hold values from -4 to 404
- rel_index: int32 [64, 64], replicated, may hold values from 0 to 224
- shifts: int32 [2, 2], P('dp'), may hold values from 1 to 7
Outputs:
- out_weight_grad: float32 [768, 1024], P('row', ('col', 'dp'))
- embed_weight_grad: float32 [48, 1024], replicated
- embed_bias_grad: float32 [1024], replicated
- norm_gain_grad: float32 [1024], replicated
- bias_table_grad: float32 [12, 225], replicated
Inputs may be any that keep to these rules, and one draw needn't show every extreme that they name: `rel_index`: each entry names one of the 225 columns of bias_table.
All inputs are finite; a program needn't handle non-finite values.
Results may differ from a plain program's by a relative error of at most 0.023.
Values may be sent and summed in bfloat16 or wider, within the bound.
No kernel may reach another device: no remote copies, remote signals or barrier semaphores. Data moves between devices by JAX's collectives and lax.ppermute only.
A program may use at most 64 MiB of HBM per device.

v0:
```python
import jax
import jax.numpy as jnp
from jax import lax
from jax.sharding import PartitionSpec as P

WIN = 8
PATCH = 4
norm_epsilon = 1e-05


def laid_out(blocks, dim):
    blocks = jnp.moveaxis(blocks, 0, dim)
    lengths = blocks.shape
    return blocks.reshape(*lengths[:dim], lengths[dim] * lengths[dim + 1], *lengths[dim + 2 :])


def gather_together(arrays, axis, dims):
    line = jnp.concatenate([a.reshape(-1) for a in arrays])
    lines, at, gathered = (lax.all_gather(line, axis), 0, [])
    for a, dim in zip(arrays, dims):
        blocks = lines[:, at : at + a.size].reshape(-1, *a.shape)
        gathered.append(laid_out(blocks, dim))
        at += a.size
    return tuple(gathered)


def from_behind(value, axis, steps):
    count = lax.axis_size(axis)
    pairs = [(source, (source + steps) % count) for source in range(count)]
    return lax.ppermute(value, axis, pairs)


def in_blocks(x, dim, length):
    before, after = (x.shape[:dim], x.shape[dim + 1 :])
    return jnp.moveaxis(x.reshape(*before, length, -1, *after), dim, 0)


def summed_on_arrival(x, axis, dim):
    blocks = in_blocks(x, dim, lax.axis_size(axis))
    arrived = lax.all_to_all(blocks, axis, split_axis=0, concat_axis=0, tiled=True)
    return arrived.astype(jnp.float32).sum(axis=0)


def summed_on_arrival_2(x, axis, dim):
    blocks = in_blocks(x, dim, lax.axis_size(axis))
    arrived = lax.all_to_all(blocks, axis, split_axis=0, concat_axis=0, tiled=True)
    return arrived.sum(axis=0)


def make_patches(pixel_block):
    images, channels, pixel_rows, pixel_cols = pixel_block.shape
    grid_rows = pixel_rows // PATCH
    grid_cols = pixel_cols // PATCH
    shaped = pixel_block.reshape(images, channels, grid_rows, PATCH, grid_cols, PATCH)
    return shaped.transpose(0, 2, 4, 1, 3, 5).reshape(
        images, grid_rows, grid_cols, channels * PATCH * PATCH
    )


def embed_cells(patches, embed_weight, embed_bias):
    return (jnp.dot(patches, embed_weight, preferred_element_type=jnp.float32) + embed_bias).astype(
        jnp.bfloat16
    )


def window_split(block):
    rows_all, cols_all, features = block.shape
    shaped = block.reshape(rows_all // WIN, WIN, cols_all // WIN, WIN, features)
    return shaped.transpose(0, 2, 1, 3, 4).reshape(-1, WIN * WIN, features)


def window_join(windows, rows_all, cols_all):
    features = windows.shape[-1]
    shaped = windows.reshape(rows_all // WIN, cols_all // WIN, WIN, WIN, features)
    return shaped.transpose(0, 2, 1, 3, 4).reshape(rows_all, cols_all, features)


def splice_after(own_block, borrowed, offsets, along_dim):
    length = own_block.shape[along_dim]

    def single(own_item, borrowed_item, offset):
        joined = jnp.concatenate([own_item, borrowed_item], along_dim - 1)
        return lax.dynamic_slice_in_dim(joined, offset, length, along_dim - 1)

    return jax.vmap(single)(own_block, borrowed, offsets)


def attend_forward(cell_windows, labels, layer_norm_gain, qkv_full, bias_full):
    window_count, cell_count, features = cell_windows.shape
    head_count = bias_full.shape[0]
    inner_width = qkv_full.shape[1] // 3
    head_size = inner_width // head_count
    score_scale = head_size ** (-0.5)
    flat_rows = cell_windows.reshape(-1, features).astype(jnp.float32)
    average = jnp.mean(flat_rows, axis=-1, keepdims=True)
    centered_input = flat_rows - average
    inverse_deviation = lax.rsqrt(
        jnp.mean(centered_input * centered_input, axis=-1, keepdims=True) + norm_epsilon
    )
    standardized_rows = centered_input * inverse_deviation
    normalized_rows = (standardized_rows * layer_norm_gain).astype(jnp.bfloat16)
    projected = jnp.dot(normalized_rows, qkv_full, preferred_element_type=jnp.float32).astype(
        jnp.bfloat16
    )
    head_shape = (window_count, cell_count, head_count, head_size)
    query_rows = projected[:, :inner_width].reshape(head_shape)
    key_vectors = projected[:, inner_width : 2 * inner_width].reshape(head_shape)
    value_rows = projected[:, 2 * inner_width :].reshape(head_shape)
    scores = (
        jnp.einsum("wmhd,wnhd->whmn", query_rows, key_vectors, preferred_element_type=jnp.float32)
        * score_scale
        + bias_full[None]
    )
    same_region = labels[:, None, :, None] == labels[:, None, None, :]
    scores = jnp.where(same_region, scores, -1e30)
    row_peak = jnp.max(scores, axis=-1, keepdims=True)
    exp_scores = jnp.exp(scores - row_peak)
    attention_weights = exp_scores / jnp.sum(exp_scores, axis=-1, keepdims=True)
    reduced_probability = attention_weights.astype(jnp.bfloat16)
    attended = jnp.einsum(
        "whmn,wnhd->wmhd", reduced_probability, value_rows, preferred_element_type=jnp.float32
    ).astype(jnp.bfloat16)
    stored_residuals = (
        standardized_rows,
        inverse_deviation,
        query_rows,
        key_vectors,
        value_rows,
        attention_weights,
        reduced_probability,
    )
    return (stored_residuals, attended.reshape(-1, inner_width))


def attend_backward(stored_residuals, d_attended, layer_norm_gain, qkv_full):
    (
        standardized_rows,
        inverse_deviation,
        query_rows,
        key_vectors,
        value_rows,
        attention_weights,
        reduced_probability,
    ) = stored_residuals
    head_shape = query_rows.shape
    score_scale = head_shape[3] ** (-0.5)
    total_row_count = standardized_rows.shape[0]
    inner_width = head_shape[2] * head_shape[3]
    d_heads = d_attended.reshape(head_shape)
    d_prob = jnp.einsum("wmhd,wnhd->whmn", d_heads, value_rows, preferred_element_type=jnp.float32)
    d_values = jnp.einsum(
        "whmn,wmhd->wnhd", reduced_probability, d_heads, preferred_element_type=jnp.float32
    ).astype(jnp.bfloat16)
    d_scores = attention_weights * (
        d_prob - jnp.sum(attention_weights * d_prob, axis=-1, keepdims=True)
    )
    table_part = jnp.sum(d_scores, axis=0)
    d_low = d_scores.astype(jnp.bfloat16)
    d_queries = (
        jnp.einsum("whmn,wnhd->wmhd", d_low, key_vectors, preferred_element_type=jnp.float32)
        * score_scale
    ).astype(jnp.bfloat16)
    d_keys = (
        jnp.einsum("whmn,wmhd->wnhd", d_low, query_rows, preferred_element_type=jnp.float32)
        * score_scale
    ).astype(jnp.bfloat16)
    d_projected = jnp.concatenate(
        [
            d_queries.reshape(total_row_count, inner_width),
            d_keys.reshape(total_row_count, inner_width),
            d_values.reshape(total_row_count, inner_width),
        ],
        axis=1,
    )
    normalized_gradient = lax.dot_general(
        d_projected, qkv_full, (((1,), (1,)), ((), ())), preferred_element_type=jnp.float32
    )
    gain_contribution = jnp.sum(normalized_gradient * standardized_rows, axis=0)
    scaled_rows = normalized_gradient * layer_norm_gain
    branch_gradient = inverse_deviation * (
        scaled_rows
        - jnp.mean(scaled_rows, axis=-1, keepdims=True)
        - standardized_rows * jnp.mean(scaled_rows * standardized_rows, axis=-1, keepdims=True)
    )
    return (branch_gradient.astype(jnp.bfloat16), gain_contribution, table_part)


def on_device(
    pixels,
    cotangent,
    embed_weight,
    embed_bias,
    layer_norm_gain,
    qkv_weight,
    out_weight,
    bias_table,
    rel_index,
    shifts,
):
    images, rows_dev, cols_dev, features = cotangent.shape
    head_count = bias_table.shape[0]
    grid_rows = rows_dev * lax.axis_size("row")
    grid_cols = cols_dev * lax.axis_size("col")
    row_shift = shifts[:, 0]
    col_shift = shifts[:, 1]
    qkv_columns, out_columns = gather_together((qkv_weight, out_weight), ("col", "dp"), (1, 1))
    qkv_full = lax.all_gather(qkv_columns, "row", axis=0, tiled=True)
    patches = make_patches(pixels)
    below = from_behind((pixels, cotangent), "row", -1)
    moved_pixels = splice_after(pixels, below[0], row_shift * PATCH, 2)
    shifted_cot = splice_after(cotangent, below[1], row_shift, 1)
    beside = from_behind((moved_pixels[:, :, :, : WIN * PATCH], shifted_cot[:, :, :WIN]), "col", -1)
    moved_pixels = splice_after(moved_pixels, beside[0], col_shift * PATCH, 3)
    shifted_cot = splice_after(shifted_cot, beside[1], col_shift, 2)
    moved_patches = make_patches(moved_pixels)
    shifted = embed_cells(moved_patches, embed_weight, embed_bias)
    row_ids = lax.axis_index("row") * rows_dev + jnp.arange(rows_dev, dtype=jnp.int32)
    col_ids = lax.axis_index("col") * cols_dev + jnp.arange(cols_dev, dtype=jnp.int32)
    row_part = (row_ids[None, :] >= grid_rows - row_shift[:, None]).astype(jnp.int32)
    col_part = (col_ids[None, :] >= grid_cols - col_shift[:, None]).astype(jnp.int32)
    region = 2 * row_part[:, :, None] + col_part[:, None, :]
    labels = window_split(region.reshape(images * rows_dev, cols_dev, 1))[:, :, 0]
    cell_windows = window_split(shifted.reshape(images * rows_dev, cols_dev, features))
    cot_flat = window_split(shifted_cot.reshape(images * rows_dev, cols_dev, features)).reshape(
        -1, features
    )
    selector = (
        rel_index.reshape(-1)[:, None] == jnp.arange(bias_table.shape[1], dtype=jnp.int32)[None, :]
    ).astype(jnp.float32)
    bias_full = jnp.dot(selector, bias_table.T, precision=lax.Precision.HIGHEST).T.reshape(
        head_count, WIN * WIN, WIN * WIN
    )
    stored_residuals, attended = attend_forward(
        cell_windows, labels, layer_norm_gain, qkv_full, bias_full
    )
    d_attended = lax.dot_general(
        cot_flat,
        lax.all_gather(out_columns, "row", axis=0, tiled=True),
        (((1,), (1,)), ((), ())),
        preferred_element_type=jnp.float32,
    ).astype(jnp.bfloat16)
    partial_rows = summed_on_arrival(
        lax.dot_general(
            attended, cot_flat, (((0,), (0,)), ((), ())), preferred_element_type=jnp.float32
        ).astype(jnp.bfloat16),
        "row",
        0,
    )
    out_weight_grad = summed_on_arrival_2(partial_rows, ("col", "dp"), 1)
    d_rows, gain_contribution, table_part = attend_backward(
        stored_residuals, d_attended, layer_norm_gain, qkv_full
    )
    branch_gradient = window_join(
        d_rows.reshape(-1, WIN * WIN, features), images * rows_dev, cols_dev
    ).reshape(images, rows_dev, cols_dev, features)
    patch_rows = patches.reshape(-1, patches.shape[-1])
    cot_rows = cotangent.reshape(-1, features)
    contract = (((0,), (0,)), ((), ()))
    branch_patches = moved_patches.reshape(-1, patches.shape[-1])
    back_rows = branch_gradient.reshape(-1, features)
    embed_grad = lax.dot_general(
        patch_rows, cot_rows, contract, preferred_element_type=jnp.float32
    ) + lax.dot_general(branch_patches, back_rows, contract, preferred_element_type=jnp.float32)
    bias_grad = jnp.sum(cot_rows, axis=0, dtype=jnp.float32) + jnp.sum(
        back_rows, axis=0, dtype=jnp.float32
    )
    table_grad = jnp.dot(
        table_part.reshape(head_count, -1), selector, precision=lax.Precision.HIGHEST
    )
    totals = lax.psum((embed_grad, bias_grad, gain_contribution, table_grad), ("row", "col", "dp"))
    return (out_weight_grad, totals[0], totals[1], totals[2], totals[3])


def solution(mesh):
    return jax.shard_map(
        on_device,
        mesh=mesh,
        in_specs=(
            P("dp", None, "row", "col"),
            P("dp", "row", "col", None),
            P(),
            P(),
            P(),
            P("row", ("col", "dp")),
            P("row", ("col", "dp")),
            P(),
            P(),
            P("dp", None),
        ),
        out_specs=(P("row", ("col", "dp")), P(), P(), P(), P()),
        check_vma=False,
    )
```

profile of v0, /device:TPU:1, one launch (start us, length us, event | category | flops | bytes accessed | tf_op | source)
XLA Modules:
  0.0 531.4 jit_solution(17640539228730412857)
XLA Ops:
  8.9 54.6 %all-gather = bf16[98304]{0:T(1024)(128)(2,1)S(1)} all-gather(bf16[6144]{0:T(1024)(128)(2,1)S(1)} %pad_maximum_fusion), channel_id=2, replica_groups=mesh['row'=32,'col'=8,'dp'=2] {'col','dp'}, dimensions={0}, use_global_device_ids=true | all-gather | bytes 208896 | tf_op jit(solution)/shard_map/all_gather | solution.py:19
  65.3 10.1 %collective-permute-start = (bf16[1,3,32,128]{3,2,1,0:T(8,128)(2,1)S(1)}, bf16[1,3,32,128]{3,2,1,0:T(8,128)(2,1)S(1)}, u32[]{:S(2)}, u32[]{:S(2)}) collective-permute-start(bf16[1,3,32,128]{3,2,1,0:T(8,128)(2,1)S(1)} %copy-done.12), channel_id=1, source_target_pairs={{0,496},{16,0},{32,16},{48,32},{64,48},{80,64},{96,80},{112,96},{1... | collective-permute-start | bytes 73736 | tf_op jit(solution)/shard_map/ppermute | solution.py:30
  75.4 1.9 collective-permute-start.2
  82.9 2.6 convolution_bitcast_fusion
  87.2 1.9 collective-permute-start.1
  98.8 2.1 collective-permute-start.3
  102.7 2.3 collective-permute-done.3
  106.1 26.1 %all-gather.4.cloned.1.call-done = bf16[1024,2304]{1,0:T(8,128)(2,1)} async-done(((bf16[32,2304]{1,0:T(8,128)(2,1)}), bf16[1024,2304]{1,0:T(8,128)(2,1)}) %all-gather.4.cloned.1.call-update) | async-done | bytes 4718608 | tf_op jit(solution)/shard_map/all_gather | solution.py:207
  132.1 3.9 convolution_convert_fusion
  138.5 2.6 reshape.338
  146.5 3.8 fusion.7
  153.3 2.9 convolution_convert_fusion.1
  156.2 5.3 all-to-all-start
  161.4 41.0 %all-gather.6.cloned.1.call-done = bf16[768,1024]{1,0:T(8,128)(2,1)} async-done(((bf16[24,1024]{1,0:T(8,128)(2,1)}), bf16[768,1024]{1,0:T(8,128)(2,1)}) %all-gather.6.cloned.1.call-update) | async-done | bytes 1572880 | tf_op jit(solution)/shard_map/all_gather | solution.py:238
  202.5 2.8 convolution_convert_fusion.4
  205.2 2.4 reshape.341
  209.5 2.5 multiply_reduce_fusion
  213.3 1.9 copy.200
  215.2 1.8 reshape.216
  225.6 2.5 fusion.8
  229.3 4.0 multiply_reduce_fusion.1
  237.9 9.8 %all-to-all-start.1 = ((f32[16,1,1536]{2,1,0:T(1,128)}), f32[16,1,1536]{2,1,0:T(1,128)S(1)}, u32[]{:S(2)}, u32[]{:S(2)}) async-start(f32[16,1,1536]{2,1,0:T(1,128)} %reshape.342), calls=%async_computation.1 | async-start | bytes 196608 | tf_op jit(solution)/shard_map/all_to_all | solution.py:46
  249.4 100.0 %all-reduce.2 = (f32[1024]{0:T(1024)}, f32[1024]{0:T(1024)}, f32[12,225]{1,0:T(8,128)}) all-reduce(f32[1024]{0:T(1024)S(1)} %add.126, f32[1024]{0:T(1024)S(1)} %get-tuple-element.49, f32[12,225]{1,0:T(8,128)S(1)} %fusion.1), channel_id=1, replica_groups=mesh['row'=32,'col'=8,'dp'=2] {'row','col','dp'}, use_global_device_ids=true, to_apply=%region_12.13 | all-reduce | flops 4748 | bytes 37984 | tf_op jit(solution)/shard_map/psum | solution.py:270
  351.4 171.8 %all-reduce.5.cloned.1.call-done = f32[48,1024]{1,0:T(8,128)} async-done(((f32[48,1024]{1,0:T(8,128)}), f32[48,1024]{1,0:T(8,128)}) %all-reduce.5.cloned.1.call-update) | async-done | bytes 196624 | tf_op jit(solution)/shard_map/psum | solution.py:270
  (132 shorter events, 50.0 us)
Async XLA Ops:
  7.2 89.5 %copy-start = (bf16[48,1024]{1,0:T(8,128)(2,1)S(1)}, bf16[48,1024]{1,0:T(8,128)(2,1)}, u32[]{:S(2)}) copy-start(bf16[48,1024]{1,0:T(8,128)(2,1)} %param.12) | copy-start | bytes 294916
  7.2 58.1 %copy-start.12 = (bf16[1,3,32,128]{3,2,1,0:T(8,128)(2,1)S(1)}, bf16[1,3,32,128]{3,2,1,0:T(8,128)(2,1)}, u32[]{:S(2)}) copy-start(bf16[1,3,32,128]{3,2,1,0:T(8,128)(2,1)} %param.10) | copy-start | bytes 73732
  7.2 68.2 %copy-start.3 = (bf16[1,8,32,1024]{3,2,1,0:T(8,128)(2,1)S(1)}, bf16[1,8,32,1024]{3,2,1,0:T(8,128)(2,1)}, u32[]{:S(2)}) copy-start(bf16[1,8,32,1024]{3,2,1,0:T(8,128)(2,1)} %param.11) | copy-start | bytes 1572868
  7.2 124.9 %all-gather.4.cloned.1.call-start = ((), (), s32[]{:S(2)}) async-start(), calls=%async_computation.2 | async-start | bytes 4866048 | tf_op jit(solution)/shard_map/all_gather | solution.py:207
  63.6 16.3 %copy-start.19 = (s32[1,2]{1,0:T(1,128)S(1)}, s32[1,2]{1,0:T(1,128)}, u32[]{:S(2)}) copy-start(s32[1,2]{1,0:T(1,128)} %param.19) | copy-start | bytes 28
  63.6 18.4 %copy-start.14 = (s32[64,64]{1,0:T(8,128)S(1)}, s32[64,64]{1,0:T(8,128)}, u32[]{:S(2)}) copy-start(s32[64,64]{1,0:T(8,128)} %param.18) | copy-start | bytes 49156
  64.2 18.7 %copy-start.20 = (f32[12,225]{1,0:T(8,128)S(1)}, f32[12,225]{1,0:T(8,128)}, u32[]{:S(2)}) copy-start(f32[12,225]{1,0:T(8,128)} %param.17) | copy-start | bytes 32404
  65.2 137.2 %all-gather.6.cloned.1.call-start = ((), (), s32[]{:S(2)}) async-start(), calls=%async_computation.3 | async-start | bytes 1622016 | tf_op jit(solution)/shard_map/all_gather | solution.py:238
  65.3 21.8 %collective-permute-start = (bf16[1,3,32,128]{3,2,1,0:T(8,128)(2,1)S(1)}, bf16[1,3,32,128]{3,2,1,0:T(8,128)(2,1)S(1)}, u32[]{:S(2)}, u32[]{:S(2)}) collective-permute-start(bf16[1,3,32,128]{3,2,1,0:T(8,128)(2,1)S(1)} %copy-done.12), channel_id=1, source_target_pairs={{0,496},{16,0},{32,16},{48,32},{64,48},{80,64},{96,80},{112,96},{1... | collective-permute-start | bytes 73736 | tf_op jit(solution)/shard_map/ppermute | solution.py:30
  75.4 22.3 %collective-permute-start.2 = (bf16[1,8,32,1024]{3,2,1,0:T(8,128)(2,1)S(1)}, bf16[1,8,32,1024]{3,2,1,0:T(8,128)(2,1)}, u32[]{:S(2)}, u32[]{:S(2)}) collective-permute-start(bf16[1,8,32,1024]{3,2,1,0:T(8,128)(2,1)S(1)} %copy-done.3), channel_id=1, source_target_pairs={{0,496},{16,0},{32,16},{48,32},{64,48},{80,64},{96,80},{112,96},{1... | collective-permute-start | bytes 1572872 | tf_op jit(solution)/shard_map/ppermute | solution.py:30
  82.1 5.1 copy-start.16
  87.2 6.9 %collective-permute-start.1 = (bf16[1,3,32,32]{3,2,1,0:T(8,128)(2,1)S(1)}, bf16[1,3,32,32]{3,2,1,0:T(8,128)(2,1)S(1)}, u32[]{:S(2)}, u32[]{:S(2)}) collective-permute-start(bf16[1,3,32,32]{3,2,1,0:T(8,128)(2,1)S(1)} %bitcast.126), channel_id=1, source_target_pairs={{0,14},{2,0},{4,2},{6,4},{8,6},{10,8},{12,10},{14,12},{1,15},{3,1}... | collective-permute-start | bytes 18440 | tf_op jit(solution)/shard_map/ppermute | solution.py:30
  92.5 4.1 copy-start.18
  97.3 3.6 copy-start.15
  98.8 6.1 %collective-permute-start.3 = (bf16[1,8,8,1024]{3,2,1,0:T(8,128)(2,1)S(1)}, bf16[1,8,8,1024]{3,2,1,0:T(8,128)(2,1)S(1)}, u32[]{:S(2)}, u32[]{:S(2)}) collective-permute-start(bf16[1,8,8,1024]{3,2,1,0:T(8,128)(2,1)S(1)} %slice.121), channel_id=1, source_target_pairs={{0,14},{2,0},{4,2},{6,4},{8,6},{10,8},{12,10},{14,12},{1,15},{3,1}... | collective-permute-start | bytes 393224 | tf_op jit(solution)/shard_map/ppermute | solution.py:30
  138.5 2.6 copy-start.5
  156.2 46.3 %copy-start.4 = (bf16[1,4,8,8,1024]{4,3,2,1,0:T(8,128)(2,1)S(1)}, bf16[1,4,8,8,1024]{4,3,2,1,0:T(8,128)(2,1)}, u32[]{:S(2)}) copy-start(bf16[1,4,8,8,1024]{4,3,2,1,0:T(8,128)(2,1)} %copy.180) | copy-start | bytes 1572868
  156.2 79.0 %all-to-all-start = ((bf16[32,24,1024]{2,1,0:T(8,128)(2,1)}), bf16[32,24,1024]{2,1,0:T(8,128)(2,1)}, u32[]{:S(2)}, u32[]{:S(2)}) async-start(bf16[32,24,1024]{2,1,0:T(8,128)(2,1)} %bitcast.113), calls=%async_computation | async-start | bytes 3145728 | tf_op jit(solution)/shard_map/all_to_all | solution.py:40
  209.5 2.6 copy-start.6
  222.8 2.8 copy-start.7
  235.2 12.6 %copy-start.11 = (f32[12,4096]{1,0:T(8,128)S(1)}, f32[12,4096]{1,0:T(8,128)}, u32[]{:S(2)}) copy-start(f32[12,4096]{1,0:T(8,128)} %reshape.216) | copy-start | bytes 589828
  235.2 12.6 %copy-start.17 = (s32[4096]{0:T(1024)S(1)}, s32[4096]{0:T(1024)}, u32[]{:S(2)}) copy-start(s32[4096]{0:T(1024)} %copy-done.16) | copy-start | bytes 49156
  237.9 111.5 %all-to-all-start.1 = ((f32[16,1,1536]{2,1,0:T(1,128)}), f32[16,1,1536]{2,1,0:T(1,128)S(1)}, u32[]{:S(2)}, u32[]{:S(2)}) async-start(f32[16,1,1536]{2,1,0:T(1,128)} %reshape.342), calls=%async_computation.1 | async-start | bytes 196608 | tf_op jit(solution)/shard_map/all_to_all | solution.py:46
  247.7 275.5 %all-reduce.5.cloned.1.call-start = ((), (), s32[]{:S(2)}) async-start(), calls=%async_computation.4 | async-start | bytes 393216 | tf_op jit(solution)/shard_map/psum | solution.py:270
  (6 other events, 8.3 us)
Sparse Core Ops, SparseCore 0:
  65.4 66.7 all-gather.3
  134.3 68.1 all-gather.5
  254.1 269.1 all-reduce.4
where the time goes:
time: 532 us; the launch traced here: 531 us
  waiting for transfers between devices  241 us (45%)
  blocking collectives  155 us (29%)
  local copies, waits for them, and re-layouts  41.8 us (8%)
  matrix products  32 us (6%)
  starting transfers between devices  31.2 us (6%)
  between operations  20.9 us (4%)
  other arithmetic  9.74 us (2%)
    psum x1, waiting for transfers between devices, on_device(): lax.psum((embed_grad, bias_grad, gain_contribution, table_grad), ('row',...  172 us
    psum x1, blocking collectives, on_device(): lax.psum((embed_grad, bias_grad, gain_contribution, table_grad), ('row',...  100 us
    all_gather x1, blocking collectives, gather_together(): lines, at, gathered = (lax.all_gather(line, axis), 0, [])  54.6 us
    all_gather x1, waiting for transfers between devices, on_device(): lax.all_gather(out_columns, 'row', axis=0, tiled=True)  41 us
    all_gather x1, waiting for transfers between devices, on_device(): qkv_full = lax.all_gather(qkv_columns, 'row', axis=0, tiled=True)  26.1 us
    ppermute x4, starting transfers between devices, from_behind(): return lax.ppermute(value, axis, pairs)  16 us
  transfers between devices with their start and end apart: 9, of which 4 were waited for; matrix products, arithmetic and copies ran while one was open for 14% of the time, Pallas kernels for 0%

commit v1 on v0

--- a/solution.py
+++ b/solution.py
@@ -235,7 +235,9 @@
     )
     d_attended = lax.dot_general(
         cot_flat,
-        lax.all_gather(out_columns, "row", axis=0, tiled=True),
+        jnp.concatenate(
+            lax.all_to_all(jnp.stack([out_columns] * lax.axis_size("row")), "row", 0, 0), axis=0
+        ),
         (((1,), (1,)), ((), ())),
         preferred_element_type=jnp.float32,
     ).astype(jnp.bfloat16)

time: 532 us -> 515 us (0.968)
  waiting for transfers between devices: 241 us -> 215 us
  starting transfers between devices: 31.2 us -> 37.8 us
    all_gather x1 -> x0, waiting for transfers between devices: 41 us -> none  [on_device(): lax.all_gather(out_columns, 'row', axis=0, tiled=True)]
    all_gather x1, waiting for transfers between devices: 26.1 us -> 35.8 us  [on_device(): qkv_full = lax.all_gather(qkv_columns, 'row', axis=0, tiled=True)]
    all_to_all x0 -> x1, starting transfers between devices: none -> 7.61 us  [on_device(): lax.all_to_all(jnp.stack([out_columns] * lax.axis_size('row')), 'row', 0, 0)]
  transfers between devices with their start and end apart: 9 -> 9, of which waited for: 4 -> 4; matrix products, arithmetic and copies ran while one was open for 14% -> 15% of each run, Pallas kernels for 0% -> 0%
where the time goes in v1:
time: 515 us; the launch traced here: 514 us
  waiting for transfers between devices  215 us (42%)
  blocking collectives  155 us (30%)
  local copies, waits for them, and re-layouts  42.5 us (8%)
  starting transfers between devices  37.8 us (7%)
  matrix products  32 us (6%)
  between operations  21.2 us (4%)
  other arithmetic  9.69 us (2%)
    psum x1, waiting for transfers between devices, on_device(): lax.psum((embed_grad, bias_grad, gain_contribution, table_grad), ('row',...  173 us
    psum x1, blocking collectives, on_device(): lax.psum((embed_grad, bias_grad, gain_contribution, table_grad), ('row',...  100 us
    all_gather x1, blocking collectives, gather_together(): lines, at, gathered = (lax.all_gather(line, axis), 0, [])  54.6 us
    all_gather x1, waiting for transfers between devices, on_device(): qkv_full = lax.all_gather(qkv_columns, 'row', axis=0, tiled=True)  35.8 us
    ppermute x4, starting transfers between devices, from_behind(): return lax.ppermute(value, axis, pairs)  16 us
  transfers between devices with their start and end apart: 9, of which 4 were waited for; matrix products, arithmetic and copies ran while one was open for 15% of the time, Pallas kernels for 0%

profile of v1, /device:TPU:1, one launch (start us, length us, event | category | flops | bytes accessed | tf_op | source)
XLA Modules:
  0.0 513.5 jit_solution(8833612063550582381)
XLA Ops:
  8.9 54.6 %all-gather = bf16[98304]{0:T(1024)(128)(2,1)S(1)} all-gather(bf16[6144]{0:T(1024)(128)(2,1)S(1)} %pad_maximum_fusion), channel_id=2, replica_groups=mesh['row'=32,'col'=8,'dp'=2] {'col','dp'}, dimensions={0}, use_global_device_ids=true | all-gather | bytes 208896 | tf_op jit(solution)/shard_map/all_gather | solution.py:19
  65.2 10.1 %collective-permute-start = (bf16[1,3,32,128]{3,2,1,0:T(8,128)(2,1)S(1)}, bf16[1,3,32,128]{3,2,1,0:T(8,128)(2,1)S(1)}, u32[]{:S(2)}, u32[]{:S(2)}) collective-permute-start(bf16[1,3,32,128]{3,2,1,0:T(8,128)(2,1)S(1)} %copy-done.12), channel_id=1, source_target_pairs={{0,496},{16,0},{32,16},{48,32},{64,48},{80,64},{96,80},{112,96},{1... | collective-permute-start | bytes 73736 | tf_op jit(solution)/shard_map/ppermute | solution.py:30
  75.3 1.9 collective-permute-start.2
  79.0 7.6 %all-to-all-start.2 = ((bf16[32,24,1024]{2,1,0:T(8,128)(2,1)}), bf16[32,24,1024]{2,1,0:T(8,128)(2,1)}, u32[]{:S(2)}, u32[]{:S(2)}) async-start(bf16[32,24,1024]{2,1,0:T(8,128)(2,1)} %stack.3), calls=%async_computation.2 | async-start | bytes 3145728 | tf_op jit(solution)/shard_map/all_to_all | solution.py:239
  91.2 2.6 convolution_bitcast_fusion
  95.6 1.9 collective-permute-start.1
  107.1 2.1 collective-permute-start.3
  111.0 2.8 collective-permute-done.3
  114.9 35.8 %all-gather.3.cloned.1.call-done = bf16[1024,2304]{1,0:T(8,128)(2,1)} async-done(((bf16[32,2304]{1,0:T(8,128)(2,1)}), bf16[1024,2304]{1,0:T(8,128)(2,1)}) %all-gather.3.cloned.1.call-update) | async-done | bytes 4718608 | tf_op jit(solution)/shard_map/all_gather | solution.py:207
  150.6 3.9 convolution_convert_fusion
  157.0 2.6 reshape.340
  165.1 3.8 fusion.7
  171.8 2.9 convolution_convert_fusion.1
  174.7 5.5 %all-to-all-start = ((bf16[32,24,1024]{2,1,0:T(8,128)(2,1)}), bf16[32,24,1024]{2,1,0:T(8,128)(2,1)}, u32[]{:S(2)}, u32[]{:S(2)}) async-start(bf16[32,24,1024]{2,1,0:T(8,128)(2,1)} %bitcast.114), calls=%async_computation | async-start | bytes 3145728 | tf_op jit(solution)/shard_map/all_to_all | solution.py:40
  180.2 2.8 convolution_convert_fusion.4
  183.0 2.4 reshape.343
  187.3 2.5 multiply_reduce_fusion
  191.1 1.9 copy.200
  203.4 2.5 fusion.8
  207.1 4.0 multiply_reduce_fusion.1
  212.9 4.2 all-to-all-done
  219.8 8.6 %all-to-all-start.1 = ((f32[16,1,1536]{2,1,0:T(1,128)}), f32[16,1,1536]{2,1,0:T(1,128)S(1)}, u32[]{:S(2)}, u32[]{:S(2)}) async-start(f32[16,1,1536]{2,1,0:T(1,128)} %reshape.344), calls=%async_computation.1 | async-start | bytes 196608 | tf_op jit(solution)/shard_map/all_to_all | solution.py:46
  230.0 100.3 %all-reduce.2 = (f32[1024]{0:T(1024)}, f32[1024]{0:T(1024)}, f32[12,225]{1,0:T(8,128)}) all-reduce(f32[1024]{0:T(1024)S(1)} %add.126, f32[1024]{0:T(1024)S(1)} %get-tuple-element.49, f32[12,225]{1,0:T(8,128)S(1)} %fusion.1), channel_id=1, replica_groups=mesh['row'=32,'col'=8,'dp'=2] {'row','col','dp'}, use_global_device_ids=true, to_apply=%region_12.13 | all-reduce | flops 4748 | bytes 37984 | tf_op jit(solution)/shard_map/psum | solution.py:272
  332.5 172.6 %all-reduce.5.cloned.1.call-done = f32[48,1024]{1,0:T(8,128)} async-done(((f32[48,1024]{1,0:T(8,128)}), f32[48,1024]{1,0:T(8,128)}) %all-reduce.5.cloned.1.call-update) | async-done | bytes 196624 | tf_op jit(solution)/shard_map/psum | solution.py:272
  (132 shorter events, 52.5 us)
Async XLA Ops:
  7.2 97.8 %copy-start = (bf16[48,1024]{1,0:T(8,128)(2,1)S(1)}, bf16[48,1024]{1,0:T(8,128)(2,1)}, u32[]{:S(2)}) copy-start(bf16[48,1024]{1,0:T(8,128)(2,1)} %param.12) | copy-start | bytes 294916
  7.2 58.0 %copy-start.12 = (bf16[1,3,32,128]{3,2,1,0:T(8,128)(2,1)S(1)}, bf16[1,3,32,128]{3,2,1,0:T(8,128)(2,1)}, u32[]{:S(2)}) copy-start(bf16[1,3,32,128]{3,2,1,0:T(8,128)(2,1)} %param.10) | copy-start | bytes 73732
  7.2 68.1 %copy-start.3 = (bf16[1,8,32,1024]{3,2,1,0:T(8,128)(2,1)S(1)}, bf16[1,8,32,1024]{3,2,1,0:T(8,128)(2,1)}, u32[]{:S(2)}) copy-start(bf16[1,8,32,1024]{3,2,1,0:T(8,128)(2,1)} %param.11) | copy-start | bytes 1572868
  7.2 143.4 %all-gather.3.cloned.1.call-start = ((), (), s32[]{:S(2)}) async-start(), calls=%async_computation.3 | async-start | bytes 4866048 | tf_op jit(solution)/shard_map/all_gather | solution.py:207
  65.2 30.3 %collective-permute-start = (bf16[1,3,32,128]{3,2,1,0:T(8,128)(2,1)S(1)}, bf16[1,3,32,128]{3,2,1,0:T(8,128)(2,1)S(1)}, u32[]{:S(2)}, u32[]{:S(2)}) collective-permute-start(bf16[1,3,32,128]{3,2,1,0:T(8,128)(2,1)S(1)} %copy-done.12), channel_id=1, source_target_pairs={{0,496},{16,0},{32,16},{48,32},{64,48},{80,64},{96,80},{112,96},{1... | collective-permute-start | bytes 73736 | tf_op jit(solution)/shard_map/ppermute | solution.py:30
  75.3 30.7 %collective-permute-start.2 = (bf16[1,8,32,1024]{3,2,1,0:T(8,128)(2,1)S(1)}, bf16[1,8,32,1024]{3,2,1,0:T(8,128)(2,1)}, u32[]{:S(2)}, u32[]{:S(2)}) collective-permute-start(bf16[1,8,32,1024]{3,2,1,0:T(8,128)(2,1)S(1)} %copy-done.3), channel_id=1, source_target_pairs={{0,496},{16,0},{32,16},{48,32},{64,48},{80,64},{96,80},{112,96},{1... | collective-permute-start | bytes 1572872 | tf_op jit(solution)/shard_map/ppermute | solution.py:30
  78.9 9.3 %copy-start.19 = (s32[1,2]{1,0:T(1,128)S(1)}, s32[1,2]{1,0:T(1,128)}, u32[]{:S(2)}) copy-start(s32[1,2]{1,0:T(1,128)} %param.19) | copy-start | bytes 28
  78.9 11.4 %copy-start.14 = (s32[64,64]{1,0:T(8,128)S(1)}, s32[64,64]{1,0:T(8,128)}, u32[]{:S(2)}) copy-start(s32[64,64]{1,0:T(8,128)} %param.18) | copy-start | bytes 49156
  79.0 95.7 %all-to-all-start.2 = ((bf16[32,24,1024]{2,1,0:T(8,128)(2,1)}), bf16[32,24,1024]{2,1,0:T(8,128)(2,1)}, u32[]{:S(2)}, u32[]{:S(2)}) async-start(bf16[32,24,1024]{2,1,0:T(8,128)(2,1)} %stack.3), calls=%async_computation.2 | async-start | bytes 3145728 | tf_op jit(solution)/shard_map/all_to_all | solution.py:239
  86.6 4.7 copy-start.20
  90.4 5.1 copy-start.16
  95.6 6.9 %collective-permute-start.1 = (bf16[1,3,32,32]{3,2,1,0:T(8,128)(2,1)S(1)}, bf16[1,3,32,32]{3,2,1,0:T(8,128)(2,1)S(1)}, u32[]{:S(2)}, u32[]{:S(2)}) collective-permute-start(bf16[1,3,32,32]{3,2,1,0:T(8,128)(2,1)S(1)} %bitcast.127), channel_id=1, source_target_pairs={{0,14},{2,0},{4,2},{6,4},{8,6},{10,8},{12,10},{14,12},{1,15},{3,1}... | collective-permute-start | bytes 18440 | tf_op jit(solution)/shard_map/ppermute | solution.py:30
  100.8 4.1 copy-start.18
  105.6 3.6 copy-start.15
  107.1 6.6 %collective-permute-start.3 = (bf16[1,8,8,1024]{3,2,1,0:T(8,128)(2,1)S(1)}, bf16[1,8,8,1024]{3,2,1,0:T(8,128)(2,1)S(1)}, u32[]{:S(2)}, u32[]{:S(2)}) collective-permute-start(bf16[1,8,8,1024]{3,2,1,0:T(8,128)(2,1)S(1)} %slice.121), channel_id=1, source_target_pairs={{0,14},{2,0},{4,2},{6,4},{8,6},{10,8},{12,10},{14,12},{1,15},{3,1}... | collective-permute-start | bytes 393224 | tf_op jit(solution)/shard_map/ppermute | solution.py:30
  157.0 2.6 copy-start.5
  174.7 5.5 %copy-start.4 = (bf16[1,4,8,8,1024]{4,3,2,1,0:T(8,128)(2,1)S(1)}, bf16[1,4,8,8,1024]{4,3,2,1,0:T(8,128)(2,1)}, u32[]{:S(2)}) copy-start(bf16[1,4,8,8,1024]{4,3,2,1,0:T(8,128)(2,1)} %copy.180) | copy-start | bytes 1572868
  174.7 42.5 %all-to-all-start = ((bf16[32,24,1024]{2,1,0:T(8,128)(2,1)}), bf16[32,24,1024]{2,1,0:T(8,128)(2,1)}, u32[]{:S(2)}, u32[]{:S(2)}) async-start(bf16[32,24,1024]{2,1,0:T(8,128)(2,1)} %bitcast.114), calls=%async_computation | async-start | bytes 3145728 | tf_op jit(solution)/shard_map/all_to_all | solution.py:40
  187.2 2.5 copy-start.6
  200.6 2.8 copy-start.7
  212.9 15.5 %copy-start.11 = (f32[12,4096]{1,0:T(8,128)S(1)}, f32[12,4096]{1,0:T(8,128)}, u32[]{:S(2)}) copy-start(f32[12,4096]{1,0:T(8,128)} %reshape.218) | copy-start | bytes 589828
  212.9 15.5 %copy-start.17 = (s32[4096]{0:T(1024)S(1)}, s32[4096]{0:T(1024)}, u32[]{:S(2)}) copy-start(s32[4096]{0:T(1024)} %copy-done.16) | copy-start | bytes 49156
  219.8 110.6 %all-to-all-start.1 = ((f32[16,1,1536]{2,1,0:T(1,128)}), f32[16,1,1536]{2,1,0:T(1,128)S(1)}, u32[]{:S(2)}, u32[]{:S(2)}) async-start(f32[16,1,1536]{2,1,0:T(1,128)} %reshape.344), calls=%async_computation.1 | async-start | bytes 196608 | tf_op jit(solution)/shard_map/all_to_all | solution.py:46
  228.4 276.7 %all-reduce.5.cloned.1.call-start = ((), (), s32[]{:S(2)}) async-start(), calls=%async_computation.4 | async-start | bytes 393216 | tf_op jit(solution)/shard_map/psum | solution.py:272
  (6 other events, 8.3 us)
Sparse Core Ops, SparseCore 0:
  65.3 85.2 all-gather.2
  234.8 270.2 all-reduce.4
